TPU v7x, 128 devices: a whole 4x4x4 slice. The times are simulated.
128 devices in a mesh: rows: 32 (over y, x, core), model: 4 (over z).
Axes of the slice: x: 4, y: 4, z: 4, core: 2. Of those that a mesh axis runs over, the one named last changes fastest.
Arguments:
- weight_gate: bfloat16 [2048, 8192], P('rows', 'model'), may hold values from -0.125 to 0.125
- low_gate: bfloat16 [2048, 64], P('rows'), may hold values from -0.125 to 0.125
- high_gate: bfloat16 [64, 8192], P(None, 'model'), may hold values from -0.75 to 0.75
- weight_up: bfloat16 [2048, 8192], P('rows', 'model'), may hold values from -0.125 to 0.125
- low_up: bfloat16 [2048, 64], P('rows'), may hold values from -0.125 to 0.125
- high_up: bfloat16 [64, 8192], P(None, 'model'), may hold values from -0.75 to 0.75
- weight_down: bfloat16 [8192, 2048], P('model', 'rows'), may hold values from -0.0625 to 0.0625
- low_down: bfloat16 [8192, 64], P('model'), may hold values from -0.0625 to 0.0625
- high_down: bfloat16 [64, 2048], P(None, 'rows'), may hold values from -0.75 to 0.75
- norm_train: float32 [2048], P(('rows', 'model')), may hold values from 0.25 to 1.75
- norm_step: float32 [2048], P(('rows', 'model')), may hold values from -0.3 to 0.3
Outputs:
- final_gate: bfloat16 [8192, 2048], P('model')
- final_up: bfloat16 [8192, 2048], P('model')
- final_down: bfloat16 [2048, 8192], P(None, 'model')
- serve_norm: bfloat16 [2048], replicated
All inputs are finite; a program needn't handle non-finite values.
Results may differ from a plain program's by a relative error of at most 0.001.
Values may be sent and summed in bfloat16 or wider, within the bound.
A program may use at most 192 MiB of HBM per device.

v0:
```python
import jax
import jax.numpy as jnp
from jax import lax
from jax.sharding import Mesh
from jax.sharding import PartitionSpec as P

ROWS = ("rows_0", "rows_1", "rows_2")
ROWS_MODEL = ("rows_0", "rows_1", "rows_2", "model")
mix_rate = 0.5


def turned_gather(arrays, axis, dims):
    turned = [jnp.moveaxis(a, dim, 0) for a, dim in zip(arrays, dims)]
    both = jnp.concatenate([t.reshape(len(t), -1) for t in turned], axis=1)
    result, at, finished = (lax.all_gather(both, axis, axis=0, tiled=True), 0, [])
    for t, dim in zip(turned, dims):
        section = result[:, at : at + t[0].size].reshape(-1, *t.shape[1:])
        finished.append(jnp.moveaxis(section, 0, dim))
        at += t[0].size
    return tuple(finished)


def in_order(tiles, dim):
    dims = list(tiles.shape[1:])
    dims[dim] *= tiles.shape[0]
    return jnp.moveaxis(tiles, 0, dim).reshape(dims)


def stacked_from(array, axes, turns):
    tiles = array
    for k in turns:
        tiles = lax.all_gather(tiles, axes[k])
    done = turns[::-1]
    back = [done.index(k) for k in range(len(axes))]
    tiles = tiles.transpose(*back, *range(len(axes), tiles.ndim))
    return tiles.reshape(-1, *array.shape)


def gathered_by_axis(array, axes, turns, dim):
    return in_order(stacked_from(array, axes, turns), dim)


def local(
    weight_gate,
    low_gate,
    high_gate,
    weight_up,
    low_up,
    high_up,
    weight_down,
    low_down,
    high_down,
    norm_train,
    norm_step,
):
    result_gate = weight_gate.astype(jnp.float32) + mix_rate * jnp.dot(
        low_gate, high_gate, preferred_element_type=jnp.float32
    )
    result_up = weight_up.astype(jnp.float32) + mix_rate * jnp.dot(
        low_up, high_up, preferred_element_type=jnp.float32
    )
    result_down = weight_down.astype(jnp.float32) + mix_rate * jnp.dot(
        low_down, high_down, preferred_element_type=jnp.float32
    )
    narrow_gate, narrow_up, narrow_down = (
        result_gate.astype(jnp.bfloat16),
        result_up.astype(jnp.bfloat16),
        result_down.astype(jnp.bfloat16),
    )
    final_gate, final_up, final_down = turned_gather(
        (narrow_gate, narrow_up, narrow_down), ROWS, (0, 0, 1)
    )
    final_gate, final_up, final_down = (final_gate.T, final_up.T, final_down.T)
    serve_norm = gathered_by_axis(
        (norm_train + norm_step).astype(jnp.bfloat16), ROWS_MODEL, (0, 1, 3, 2), 0
    )
    return (final_gate, final_up, final_down, serve_norm)


def solution(mesh):
    split = Mesh(
        mesh.devices.reshape(4, 4, 2, mesh.shape["model"]), ("rows_0", "rows_1", "rows_2", "model")
    )
    placed = (
        P(ROWS, "model"),
        P(ROWS, None),
        P(None, "model"),
        P(ROWS, "model"),
        P(ROWS, None),
        P(None, "model"),
        P("model", ROWS),
        P("model", None),
        P(None, ROWS),
        P(ROWS_MODEL),
        P(ROWS_MODEL),
    )
    return jax.shard_map(
        local,
        mesh=split,
        in_specs=placed,
        out_specs=(P("model", None), P("model", None), P(None, "model"), P()),
        check_vma=False,
    )
```

profile of v0, /device:TPU:1, one launch (start us, length us, event | category | flops | bytes accessed | tf_op | source)
XLA Modules:
  0.0 156.6 jit_solution(8086940729364175655)
XLA Ops:
  7.2 0.0 copy-start
  7.2 0.0 all-gather.7.cloned.1.call-start
  7.2 0.9 copy-done
  8.1 1.2 fusion.4
  9.3 1.3 fusion.5
  10.6 1.3 fusion.6
  11.9 0.9 pad_maximum_fusion
  12.8 0.0 all-gather.7.cloned.1.call-update
  12.9 1.2 dynamic-slice
  14.8 0.7 add_convert_fusion
  15.4 0.2 dynamic-update-slice
  15.6 9.5 %all-reduce = bf16[64]{0:T(256)(128)(2,1)S(1)} all-reduce(bf16[64]{0:T(256)(128)(2,1)S(1)} %dynamic-update-slice), channel_id=2, replica_groups=mesh['rows_0'=4,'rows_1'=4,'rows_2'=2,'model'=4] {'rows_0'}, use_global_device_ids=true, to_apply=%add | all-reduce | flops 64 | bytes 256
  25.2 0.1 reshape.15
  25.2 8.7 %all-gather.4 = bf16[4,4,16]{2,1,0:T(4,128)(2,1)S(1)} all-gather(bf16[1,4,16]{2,1,0:T(4,128)(2,1)S(1)} %reshape.15), channel_id=3, replica_groups=mesh['rows_0'=4,'rows_1'=4,'rows_2'=2,'model'=4] {'rows_1'}, dimensions={0}, use_global_device_ids=true | all-gather | bytes 640 | tf_op jit(solution)/shard_map/all_gather | solution.py:32
  33.9 11.1 %all-gather.2 = bf16[16,4,16]{2,1,0:T(4,128)(2,1)S(1)} all-gather(bf16[4,4,16]{2,1,0:T(4,128)(2,1)S(1)} %all-gather.4), channel_id=4, replica_groups=mesh['rows_0'=4,'rows_1'=4,'rows_2'=2,'model'=4] {'model'}, dimensions={0}, use_global_device_ids=true | all-gather | bytes 2560 | tf_op jit(solution)/shard_map/all_gather | solution.py:32
  45.0 7.4 %all-gather.3 = bf16[8,4,4,16]{3,2,1,0:T(4,128)(2,1)S(1)} all-gather(bf16[4,4,4,16]{3,2,1,0:T(4,128)(2,1)S(1)} %bitcast.20), channel_id=5, replica_groups=mesh['rows_0'=4,'rows_1'=4,'rows_2'=2,'model'=4] {'rows_2'}, dimensions={0}, use_global_device_ids=true | all-gather | bytes 6144 | tf_op jit(solution)/shard_map/all_gather | solution.py:32
  52.4 0.7 reshape_reshape.3
  53.1 55.3 %all-gather.7.cloned.1.call-done = bf16[2048,6144]{1,0:T(8,128)(2,1)} async-done(((bf16[64,6144]{1,0:T(8,128)(2,1)}), bf16[2048,6144]{1,0:T(8,128)(2,1)}) %all-gather.7.cloned.1.call-update) | async-done | bytes 25165840 | tf_op jit(solution)/shard_map/all_gather | solution.py:15
  108.4 16.9 %fusion.7 = (bf16[2048,2048]{1,0:T(8,128)(2,1)}, bf16[2048,2048]{0,1:T(8,128)(2,1)}, bf16[2048,2048]{0,1:T(8,128)(2,1)}) fusion(bf16[2048,6144]{1,0:T(8,128)(2,1)} %all-gather.7.cloned.1.call-done), kind=kLoop, calls=%fused_computation.15 | loop fusion | bytes 50331648 | tf_op jit(solution)/shard_map/slice | solution.py:17
  125.3 12.2 %copy.21 = bf16[2048,2048]{1,0:T(8,128)(2,1)} copy(bf16[2048,2048]{0,1:T(8,128)(2,1)} %get-tuple-element.18) | data formatting | bytes 16777216
  137.5 0.0 copy-start.1
  137.5 12.3 %copy.22 = bf16[2048,2048]{1,0:T(8,128)(2,1)} copy(bf16[2048,2048]{0,1:T(8,128)(2,1)} %get-tuple-element.17) | data formatting | bytes 16777216
  149.8 0.0 copy-done.1
  (2 shorter events, 0.0 us)
Async XLA Ops:
  7.2 1.0 copy-start
  7.2 101.2 %all-gather.7.cloned.1.call-start = ((), (), s32[]{:S(2)}) async-start(), calls=%async_computation | async-start | bytes 25952256 | tf_op jit(solution)/shard_map/all_gather | solution.py:15
  137.5 12.3 %copy-start.1 = (bf16[64,2048]{1,0:T(8,128)(2,1)S(1)}, bf16[64,2048]{1,0:T(8,128)(2,1)}, u32[]{:S(2)}) copy-start(bf16[64,2048]{1,0:T(8,128)(2,1)} %param.16) | copy-start | bytes 786436
Sparse Core Ops, SparseCore 0:
  13.0 95.3 all-gather.6
where the time goes:
time: 157 us
  waiting for transfers between devices  55.3 us (35%)
  local copies, waits for them, and re-layouts  44.6 us (28%)
  blocking collectives  36.6 us (23%)
  between operations  14.7 us (9%)
  matrix products  3.75 us (2%)
  other arithmetic  1.61 us (1%)
    all_gather x1, waiting for transfers between devices, turned_gather(): lax.all_gather(both, axis, axis=0, tiled=True)  55.3 us
    all_gather x3, blocking collectives, stacked_from(): tiles = lax.all_gather(tiles, axes[k])  27.1 us
    unnamed x10, local copies, waits for them, and re-layouts  26.9 us
    slice x1, local copies, waits for them, and re-layouts, turned_gather(): section = result[:, at:at + t[0].size].reshape(-1, *t.shape[1:])  16.9 us
    unnamed x1, blocking collectives  9.52 us
  transfers between devices with their start and end apart: 1, of which 1 were waited for; matrix products, arithmetic and copies ran while one was open for 2% of the time, Pallas kernels for 0%

commit v1 on v0

--- a/solution.py
+++ b/solution.py
@@ -12,7 +12,13 @@
 def turned_gather(arrays, axis, dims):
     turned = [jnp.moveaxis(a, dim, 0) for a, dim in zip(arrays, dims)]
     both = jnp.concatenate([t.reshape(len(t), -1) for t in turned], axis=1)
-    result, at, finished = (lax.all_gather(both, axis, axis=0, tiled=True), 0, [])
+    result, at, finished = (
+        jnp.concatenate(
+            lax.all_to_all(jnp.stack([both] * lax.axis_size(axis)), axis, 0, 0), axis=0
+        ),
+        0,
+        [],
+    )
     for t, dim in zip(turned, dims):
         section = result[:, at : at + t[0].size].reshape(-1, *t.shape[1:])
         finished.append(jnp.moveaxis(section, 0, dim))

time: 157 us -> 402 us (2.56); the launches traced: 157 us -> 397 us
  blocking collectives: 36.6 us -> 331 us
  waiting for transfers between devices: 55.3 us -> 0.01 us
  between operations: 14.7 us -> 1.37 us
  starting transfers between devices: 0.04 us -> 8.76 us
  local copies, waits for them, and re-layouts: 44.6 us -> 52.6 us
    unnamed x1, blocking collectives: 9.52 us -> 298 us
    all_gather x1 -> x0, waiting for transfers between devices: 55.3 us -> none  [turned_gather(): lax.all_gather(both, axis, axis=0, tiled=True)]
    all_to_all x0 -> x1, starting transfers between devices: none -> 8.76 us  [turned_gather(): lax.all_to_all(jnp.stack([both] * lax.axis_size(axis)), axis, 0, 0)]
    another operation x0 -> x1, local copies, waits for them, and re-layouts: none -> 8.65 us  [turned_gather(): jnp.stack([both] * lax.axis_size(axis))]
    all_gather x3, blocking collectives: 27.1 us -> 32.4 us  [stacked_from(): tiles = lax.all_gather(tiles, axes[k])]
    unnamed x10 -> x16, local copies, waits for them, and re-layouts: 26.9 us -> 26.4 us
  transfers between devices with their start and end apart: 1 -> 1, of which waited for: 1 -> 0; matrix products, arithmetic and copies ran while one was open for 2% -> 0% of each run, Pallas kernels for 0% -> 0%
where the time goes in v1:
time: 402 us; the launch traced here: 397 us
  blocking collectives  331 us (82%)
  local copies, waits for them, and re-layouts  52.6 us (13%)
  starting transfers between devices  8.76 us (2%)
    unnamed x1, blocking collectives  298 us
    all_gather x3, blocking collectives, stacked_from(): tiles = lax.all_gather(tiles, axes[k])  32.4 us
    unnamed x16, local copies, waits for them, and re-layouts  26.4 us
    slice x1, local copies, waits for them, and re-layouts, turned_gather(): section = result[:, at:at + t[0].size].reshape(-1, *t.shape[1:])  16.9 us
    all_to_all x1, starting transfers between devices, turned_gather(): lax.all_to_all(jnp.stack([both] * lax.axis_size(axis)), axis, 0, 0)  8.76 us
    another operation x1, local copies, waits for them, and re-layouts, turned_gather(): jnp.stack([both] * lax.axis_size(axis))  8.65 us
  transfers between devices with their start and end apart: 1, of which 0 were waited for; matrix products, arithmetic and copies ran while one was open for 0% of the time, Pallas kernels for 0%

profile of v1, /device:TPU:1, one launch (start us, length us, event | category | flops | bytes accessed | tf_op | source)
XLA Modules:
  0.0 397.3 jit_solution(5101727194362285379)
XLA Ops:
  0.6 0.0 copy-start
  0.6 0.9 copy-done
  1.6 1.2 fusion.4
  2.8 1.3 fusion.5
  4.0 1.3 fusion.6
  5.4 0.1 pad_maximum_fusion
  5.4 8.6 %stack.2 = bf16[32,64,6144]{2,1,0:T(8,128)(2,1)} broadcast(bf16[64,6144]{1,0:T(8,128)(2,1)S(1)} %pad_maximum_fusion), dimensions={1,2} | broadcast | bytes 25952256 | tf_op jit(solution)/shard_map/stack | solution.py:17
  14.1 8.8 %all-to-all-start = ((bf16[32,64,6144]{2,1,0:T(8,128)(2,1)}), bf16[32,64,6144]{2,1,0:T(8,128)(2,1)}, u32[]{:S(2)}, u32[]{:S(2)}) async-start(bf16[32,64,6144]{2,1,0:T(8,128)(2,1)} %stack.2), calls=%async_computation | async-start | bytes 50331648 | tf_op jit(solution)/shard_map/all_to_all | solution.py:17
  22.8 0.0 copy-done.4
  22.9 0.6 dynamic-slice
  24.1 0.0 copy-done.2
  24.1 0.0 copy-done.3
  24.1 0.2 dynamic-update-slice
  24.4 298.3 %all-reduce = bf16[64]{0:T(256)(128)(2,1)S(1)} all-reduce(bf16[64]{0:T(256)(128)(2,1)S(1)} %dynamic-update-slice), channel_id=2, replica_groups=mesh['rows_0'=4,'rows_1'=4,'rows_2'=2,'model'=4] {'rows_0'}, use_global_device_ids=true, to_apply=%add | all-reduce | flops 64 | bytes 256
  322.7 0.1 reshape.21
  322.8 16.3 %all-gather.4 = bf16[4,4,16]{2,1,0:T(4,128)(2,1)S(1)} all-gather(bf16[1,4,16]{2,1,0:T(4,128)(2,1)S(1)} %reshape.21), channel_id=3, replica_groups=mesh['rows_0'=4,'rows_1'=4,'rows_2'=2,'model'=4] {'rows_1'}, dimensions={0}, use_global_device_ids=true | all-gather | bytes 640 | tf_op jit(solution)/shard_map/all_gather | solution.py:38
  339.1 10.3 %all-gather.2 = bf16[16,4,16]{2,1,0:T(4,128)(2,1)S(1)} all-gather(bf16[4,4,16]{2,1,0:T(4,128)(2,1)S(1)} %all-gather.4), channel_id=4, replica_groups=mesh['rows_0'=4,'rows_1'=4,'rows_2'=2,'model'=4] {'model'}, dimensions={0}, use_global_device_ids=true | all-gather | bytes 2560 | tf_op jit(solution)/shard_map/all_gather | solution.py:38
  349.4 5.8 %all-gather.3 = bf16[8,4,4,16]{3,2,1,0:T(4,128)(2,1)S(1)} all-gather(bf16[4,4,4,16]{3,2,1,0:T(4,128)(2,1)S(1)} %bitcast.21), channel_id=5, replica_groups=mesh['rows_0'=4,'rows_1'=4,'rows_2'=2,'model'=4] {'rows_2'}, dimensions={0}, use_global_device_ids=true | all-gather | bytes 6144 | tf_op jit(solution)/shard_map/all_gather | solution.py:38
  355.2 0.7 reshape_reshape.3
  355.9 0.0 all-to-all-done
  355.9 16.9 %fusion.7 = (bf16[2048,2048]{1,0:T(8,128)(2,1)}, bf16[2048,2048]{0,1:T(8,128)(2,1)}, bf16[2048,2048]{0,1:T(8,128)(2,1)}) fusion(bf16[2048,6144]{1,0:T(8,128)(2,1)} %bitcast.1), kind=kLoop, calls=%fused_computation.15 | loop fusion | bytes 50331648 | tf_op jit(solution)/shard_map/slice | solution.py:23
  372.8 12.2 %copy.21 = bf16[2048,2048]{1,0:T(8,128)(2,1)} copy(bf16[2048,2048]{0,1:T(8,128)(2,1)} %get-tuple-element.18) | data formatting | bytes 16777216
  385.1 12.3 %copy.22 = bf16[2048,2048]{1,0:T(8,128)(2,1)} copy(bf16[2048,2048]{0,1:T(8,128)(2,1)} %get-tuple-element.17) | data formatting | bytes 16777216
  397.3 0.0 copy-done.1
  (7 shorter events, 0.0 us)
Async XLA Ops:
  0.6 1.0 copy-start
  14.1 8.8 %copy-start.4 = (u32[128]{0:T(128)S(1)}, u32[128]{0:T(128)}, u32[]{:S(2)}) copy-start(u32[128]{0:T(128)} %constant.7) | copy-start | bytes 1540
  14.1 10.0 %copy-start.2 = (f32[16]{0:T(128)S(1)}, f32[16]{0:T(128)}, u32[]{:S(2)}) copy-start(f32[16]{0:T(128)} %param.20) | copy-start | bytes 196
  14.1 10.0 %copy-start.3 = (f32[16]{0:T(128)S(1)}, f32[16]{0:T(128)}, u32[]{:S(2)}) copy-start(f32[16]{0:T(128)} %param.21) | copy-start | bytes 196
  14.1 341.9 %all-to-all-start = ((bf16[32,64,6144]{2,1,0:T(8,128)(2,1)}), bf16[32,64,6144]{2,1,0:T(8,128)(2,1)}, u32[]{:S(2)}, u32[]{:S(2)}) async-start(bf16[32,64,6144]{2,1,0:T(8,128)(2,1)} %stack.2), calls=%async_computation | async-start | bytes 50331648 | tf_op jit(solution)/shard_map/all_to_all | solution.py:17
  385.1 12.3 %copy-start.1 = (bf16[64,2048]{1,0:T(8,128)(2,1)S(1)}, bf16[64,2048]{1,0:T(8,128)(2,1)}, u32[]{:S(2)}) copy-start(bf16[64,2048]{1,0:T(8,128)(2,1)} %param.16) | copy-start | bytes 786436
